TPU v7x, 256 devices: a whole 4x4x8 slice. The times are simulated.
256 devices in a mesh: ctx: 32 (over x, y, core), tp: 8 (over z).
Axes of the slice: x: 4, y: 4, z: 8, core: 2. Of those that a mesh axis runs over, the one named last changes fastest.
Arguments:
- patches: bfloat16 [16384, 1280], P('ctx'), may hold values from -21 to 21
- window_ids: int32 [16384], P('ctx'), may hold values from -1 to 4095, as said below
- positions: int32 [4096], P('ctx'), may hold values from 0 to 32768, as said below
- text_embed: bfloat16 [32768, 8192], P('ctx', 'tp'), may hold values from -6 to 6
- cotangent: bfloat16 [32768, 8192], P('ctx', 'tp'), may hold values from -0.119628906 to 0.119628906
- qkv_weight: bfloat16 [3, 1280, 1280], P(None, None, 'tp'), may hold values from -0.15625 to 0.15625
- out_weight: bfloat16 [1280, 1280], P('tp'), may hold values from -0.15625 to 0.15625
- merger_weight: bfloat16 [5120, 8192], P('ctx', 'tp'), may hold values from -0.078125 to 0.078125
- norm_gain: bfloat16 [8192], P('tp'), may hold values from 0.099609375 to 1.8984375
Outputs:
- normed: bfloat16 [32768, 8192], P('ctx', 'tp')
- merger_grad: float32 [5120, 8192], P('ctx', 'tp')
Inputs may be any that keep to these rules, and one draw needn't show every extreme that they name: `window_ids`: windows are runs of consecutive patch slots of one index of ctx, each of 4 to 64 slots and a multiple of 4; every window id belongs to one index of ctx; the padding slots of an index of ctx come after its live slots and carry -1. Merged slot j of an index of ctx covers its patch slots 4j to 4j+3 and is live exactly when those are; live slots carry distinct positions, dead ones carry 32768. The live slots of one index of ctx name at most 4 positions among the 1024 positions of any one index of ctx.
All inputs are finite; a program needn't handle non-finite values.
Results may differ from a plain program's by a relative error of at most 0.014.
Values may be sent and summed in bfloat16 or wider, within the bound.
A program may use at most 128 MiB of HBM per device.

v0:
```python
import jax
import jax.numpy as jnp
from jax import lax
from jax.sharding import PartitionSpec as P

D = 8192
HEAD_DIM = 80


def sent_to_all(shard, axis):
    copies = jnp.broadcast_to(shard, (lax.axis_size(axis), *shard.shape))
    return lax.all_to_all(copies, axis, split_axis=0, concat_axis=0, tiled=True)


def taken_together(shard, axis):
    return sent_to_all(shard, axis).sum(axis=0)


def in_one(arrays, axis):
    ends = [0]
    for a in arrays:
        ends.append(ends[-1] + a.size)
    so_far = taken_together(jnp.concatenate([a.ravel() for a in arrays]), axis)
    return tuple((so_far[b:e].reshape(a.shape) for a, b, e in zip(arrays, ends, ends[1:])))


def window_attention(patches, window_ids, qkv_weight):
    slot_rows = patches.shape[0]
    projected = [
        jnp.dot(patches, qkv_weight[i], preferred_element_type=jnp.float32).astype(jnp.bfloat16)
        for i in range(3)
    ]
    local_heads = qkv_weight.shape[2] // HEAD_DIM
    queries = projected[0].reshape(slot_rows, local_heads, HEAD_DIM)
    keys_all = projected[1].reshape(slot_rows, local_heads, HEAD_DIM)
    values = projected[2].reshape(slot_rows, local_heads, HEAD_DIM)
    width = min(512, slot_rows)
    factor = 1.0 / HEAD_DIM**0.5

    def one_block(block_index):
        scores = (
            jnp.einsum("qhd,khd->hqk", queries, keys_all, preferred_element_type=jnp.float32)
            * factor
        )
        allowed = (window_ids[:, None] == window_ids[None, :]) & (window_ids[None, :] >= 0)
        scores = jnp.where(allowed[None], scores, jnp.float32(-1e30))
        highest = jnp.max(scores, axis=2, keepdims=True)
        weights = jnp.exp(scores - highest)
        probs = (weights / jnp.sum(weights, axis=2, keepdims=True)).astype(jnp.bfloat16)
        attended = jnp.einsum("hqk,khd->qhd", probs, values, preferred_element_type=jnp.float32)
        return attended.astype(jnp.bfloat16).reshape(width, local_heads * HEAD_DIM)

    blocks = lax.map(one_block, jnp.arange(slot_rows // width, dtype=jnp.int32))
    return blocks.reshape(slot_rows, local_heads * HEAD_DIM)


def contract_rows(left, right):
    return lax.dot_general(
        left, right, (((0,), (0,)), ((), ())), preferred_element_type=jnp.float32
    )


def shards(
    patches,
    window_ids,
    positions,
    text_embed,
    cotangent,
    qkv_weight,
    out_weight,
    merger_weight,
    norm_gain,
):
    ctx_size = lax.axis_size("ctx")
    slots = positions.shape[0]
    tok_rows = text_embed.shape[0]
    bucket_size = slots // ctx_size
    attended = window_attention(patches, window_ids, qkv_weight)
    partial_out = jnp.dot(attended, out_weight, preferred_element_type=jnp.float32)
    summed = lax.psum(partial_out.astype(jnp.bfloat16), "tp").astype(jnp.float32)
    hidden = (patches.astype(jnp.float32) + summed).astype(jnp.bfloat16)
    merged_in = hidden.reshape(slots, 4 * hidden.shape[1])
    columns = lax.all_to_all(merged_in, "ctx", split_axis=1, concat_axis=0, tiled=True)
    chosen = merged_in
    merged = jnp.dot(
        chosen,
        lax.all_gather(merger_weight, "ctx", axis=0, tiled=True),
        preferred_element_type=jnp.float32,
    ).astype(jnp.bfloat16)
    target = positions // tok_rows
    hits = (target[:, None] == jnp.arange(ctx_size, dtype=jnp.int32)[None, :]).astype(jnp.int32)
    ranks = jnp.sum(jnp.cumsum(hits, axis=0) * hits, axis=1) - 1
    bucket = jnp.where(target < ctx_size, target * bucket_size + ranks, -1)
    select = jnp.arange(slots, dtype=jnp.int32)[:, None] == bucket[None, :]
    select_mat = select.astype(jnp.bfloat16)
    outgoing = jnp.dot(select_mat, merged, preferred_element_type=jnp.float32).astype(jnp.bfloat16)
    local_row = positions % tok_rows
    occupied = jnp.any(select, axis=1)
    out_rows = jnp.where(occupied, jnp.sum(jnp.where(select, local_row[None, :], 0), axis=1), -1)
    incoming, in_rows = (
        lax.all_to_all(outgoing, "ctx", split_axis=0, concat_axis=0, tiled=True),
        lax.all_to_all(out_rows, "ctx", split_axis=0, concat_axis=0, tiled=True),
    )
    placed = jnp.arange(tok_rows, dtype=jnp.int32)[:, None] == in_rows[None, :]
    placed_mat = placed.astype(jnp.bfloat16)
    vision = jnp.dot(placed_mat, incoming, preferred_element_type=jnp.float32)
    is_vision = jnp.any(placed, axis=1)
    embedded = jnp.where(is_vision[:, None], vision, text_embed.astype(jnp.float32))
    gain_vec = norm_gain.astype(jnp.float32)[None, :]
    gained = gain_vec * cotangent.astype(jnp.float32)
    squares, inner = in_one(
        (jnp.sum(embedded * embedded, axis=1), jnp.sum(embedded * gained, axis=1)), "tp"
    )
    scale = lax.rsqrt(squares / D + 1e-06)[:, None]
    normed = (embedded * scale * gain_vec).astype(jnp.bfloat16)
    d_embed = (scale * gained - embedded * scale**3 * inner[:, None] / D).astype(jnp.bfloat16)
    back_rows = contract_rows(placed_mat, d_embed).astype(jnp.bfloat16)
    returned = lax.all_to_all(back_rows, "ctx", split_axis=0, concat_axis=0, tiled=True)
    d_merged = contract_rows(select_mat, returned).astype(jnp.bfloat16)
    chosen = columns
    merger_grad = contract_rows(chosen, lax.all_gather(d_merged, "ctx", axis=0, tiled=True))
    return (normed, merger_grad)


def solution(mesh):
    in_specs = (
        P("ctx", None),
        P("ctx"),
        P("ctx"),
        P("ctx", "tp"),
        P("ctx", "tp"),
        P(None, None, "tp"),
        P("tp", None),
        P("ctx", "tp"),
        P("tp"),
    )
    out_specs = (P("ctx", "tp"), P("ctx", "tp"))
    return jax.shard_map(shards, mesh=mesh, in_specs=in_specs, out_specs=out_specs, check_vma=False)
```

profile of v0, /device:TPU:1, one launch (start us, length us, event | category | flops | bytes accessed | tf_op | source)
XLA Modules:
  0.0 239.2 jit_solution(6177392035362610401)
XLA Ops:
  8.1 2.1 convolution_convert_fusion.7
  10.2 2.0 convolution_convert_fusion.5
  12.2 1.6 convolution_convert_fusion.6
  15.0 1.2 convolution_convert_fusion.4
  16.3 1.6 convolution_convert_fusion
  19.9 8.6 %all-to-all-start = ((s32[32,4,1]{1,2,0:T(1,128)}), s32[32,4,1]{1,2,0:T(1,128)S(1)}, u32[]{:S(2)}, u32[]{:S(2)}) async-start(s32[32,4,1]{1,2,0:T(1,128)} %bitcast), calls=%async_computation | async-start | bytes 32768 | tf_op jit(solution)/shard_map/all_to_all | solution.py:102
  28.5 66.8 %all-reduce.2.cloned.1.call-done = bf16[512,1280]{1,0:T(8,128)(2,1)} async-done(((bf16[512,1280]{1,0:T(8,128)(2,1)}), bf16[512,1280]{1,0:T(8,128)(2,1)}) %all-reduce.2.cloned.1.call-update) | async-done | bytes 1310736 | tf_op jit(solution)/shard_map/psum | solution.py:80
  95.3 1.6 add_convert_fusion
  97.8 5.7 %convolution_convert_fusion.2 = bf16[128,1024]{1,0:T(8,128)(2,1)S(1)} fusion(bf16[128,5120]{1,0:T(8,128)(2,1)S(1)} %reshape.118, bf16[5120,1024]{1,0:T(8,128)(2,1)} %all-gather.3.cloned.1.call-done, s32[128]{0:T(128)S(1)} %compare_select_fusion), kind=kOutput, calls=%fused_computation.19 | convolution fusion | flops 1376010240 | bytes 12059136 | tf_op jit(solution)/shard_map/dot_general | solution.py:96
  104.3 11.4 %all-to-all-start.1 = ((bf16[32,4,1024]{2,1,0:T(4,128)(2,1)}), bf16[32,4,1024]{2,1,0:T(4,128)(2,1)S(1)}, u32[]{:S(2)}, u32[]{:S(2)}) async-start(bf16[32,4,1024]{2,1,0:T(4,128)(2,1)} %all_to_all.39), calls=%async_computation.1 | async-start | bytes 524288 | tf_op jit(solution)/shard_map/all_to_all | solution.py:101
  115.8 3.9 %copy.37 = bf16[1024,1024]{0,1:T(8,128)(2,1)} copy(bf16[1024,1024]{1,0:T(8,128)(2,1)} %param.13) | data formatting | bytes 4194304 | tf_op args[4]
  119.7 4.0 %copy.36 = bf16[1024,1024]{0,1:T(8,128)(2,1)} copy(bf16[1024,1024]{1,0:T(8,128)(2,1)} %param.12) | data formatting | bytes 4194304 | tf_op args[3]
  125.2 5.6 %multiply_reduce_fusion.1 = (f32[1024]{0:T(1024)S(1)}, f32[1024]{0:T(1024)S(1)}, f32[1024,1024]{0,1:T(8,128)}) fusion(bf16[1024,1024]{0,1:T(8,128)(2,1)} %copy.37, f32[1024]{0:T(1024)S(1)} %convert_element_type.78, bf16[1024,1024]{0,1:T(8,128)(2,1)} %copy.36, bf16[128,1024]{1,0:T(8,128)(2,1)S(1)} %all_to_all.41, s32[128]{0:T(128)S(1)} %eq.74, ...), kind=kOutput, calls=%fused_computation.5 | convolution fusion | flops 276953088 | bytes 8664576 | tf_op jit(solution)/shard_map/dot_general | solution.py:106
  130.9 11.2 %all_to_all.55 = f32[8,1,2048]{2,1,0:T(1,128)S(1)} all-to-all(f32[8,1,2048]{2,1,0:T(1,128)S(1)} %broadcast_in_dim.73), channel_id=1, replica_groups=mesh['ctx'=32,'tp'=8] {'tp'}, dimensions={0} | all-to-all | bytes 131072 | tf_op jit(solution)/shard_map/all_to_all | solution.py:12
  142.2 4.3 %fusion.6 = bf16[128,1024]{1,0:T(8,128)(2,1)S(1)} fusion(f32[1024,1024]{0,1:T(8,128)} %get-tuple-element.37, bf16[1024,1024]{0,1:T(8,128)(2,1)} %copy.37, f32[1024]{0:T(1024)S(1)} %get-tuple-element.34, f32[1024]{0:T(1024)S(1)} %get-tuple-element.32, f32[1024]{0:T(1024)S(1)} %get-tuple-element.33, f32[1024]{0:T(1024)S(1)} %convert_element_type.78, ...), kind=kOutput, calls=%fused_computation.17 | convolution fusion | flops 277217280 | bytes 6570496 | tf_op jit(solution)/shard_map/dot_general | solution.py:58
  146.5 17.6 %all_to_all.56 = bf16[32,4,1024]{2,1,0:T(4,128)(2,1)S(1)} all-to-all(bf16[32,4,1024]{2,1,0:T(4,128)(2,1)S(1)} %all_to_all.47), channel_id=1, replica_groups=mesh['ctx'=32,'tp'=8] {'ctx'}, dimensions={0} | all-to-all | bytes 524288 | tf_op jit(solution)/shard_map/all_to_all | solution.py:118
  165.2 3.6 %all_to_all.43 = bf16[128,32,160]{2,1,0:T(8,128)(2,1)} reshape(bf16[512,1280]{1,0:T(8,128)(2,1)S(1)} %add_convert_fusion) | data formatting | bytes 2621440 | tf_op jit(solution)/shard_map/all_to_all | solution.py:83
  168.8 4.4 %copy.39 = bf16[128,32,160]{0,2,1:T(8,128)(2,1)} copy(bf16[128,32,160]{2,1,0:T(8,128)(2,1)} %all_to_all.43) | data formatting | bytes 2621440 | tf_op jit(solution)/shard_map/all_to_all | solution.py:83
  173.2 4.5 %all-to-all-start.3 = ((bf16[128,32,160]{0,2,1:T(8,128)(2,1)}), bf16[128,32,160]{0,2,1:T(8,128)(2,1)}, u32[]{:S(2)}, u32[]{:S(2)}) async-start(bf16[128,32,160]{0,2,1:T(8,128)(2,1)} %copy.39), calls=%async_computation.3 | async-start | bytes 2621440 | tf_op jit(solution)/shard_map/all_to_all | solution.py:83
  177.7 2.6 %multiply_convert_fusion = bf16[1024,1024]{0,1:T(8,128)(2,1)S(1)} fusion(f32[1024,1024]{0,1:T(8,128)} %get-tuple-element.37, f32[1024]{0:T(1024)S(1)} %get-tuple-element.33, f32[1024]{0:T(1024)S(1)} %convert_element_type.78), kind=kLoop, calls=%fused_computation.2 | loop fusion | flops 3145728 | bytes 6299648 | tf_op jit(solution)/shard_map/convert_element_type | solution.py:115
  180.3 2.6 %copy.41 = bf16[1024,1024]{1,0:T(8,128)(2,1)} copy(bf16[1024,1024]{0,1:T(8,128)(2,1)S(1)} %multiply_convert_fusion) | data formatting | bytes 4194304
  182.9 15.3 %all-to-all-done.3 = bf16[128,32,160]{0,2,1:T(8,128)(2,1)} async-done(((bf16[128,32,160]{0,2,1:T(8,128)(2,1)}), bf16[128,32,160]{0,2,1:T(8,128)(2,1)}, u32[]{:S(2)}, u32[]{:S(2)}) %all-to-all-start.3) | async-done | bytes 1310752 | tf_op jit(solution)/shard_map/all_to_all | solution.py:83
  198.2 27.4 %all-gather.5.cloned.1.call-done = bf16[4096,1024]{1,0:T(8,128)(2,1)} async-done(((bf16[128,1024]{1,0:T(8,128)(2,1)}), bf16[4096,1024]{1,0:T(8,128)(2,1)}) %all-gather.5.cloned.1.call-update) | async-done | bytes 8388624 | tf_op jit(solution)/shard_map/all_gather | solution.py:121
  225.6 6.2 %fusion.3 = f32[160,1024]{1,0:T(8,128)} fusion(bf16[4096,1024]{1,0:T(8,128)(2,1)} %all-gather.5.cloned.1.call-done, bf16[128,32,160]{0,2,1:T(8,128)(2,1)} %all-to-all-done.3), kind=kOutput, calls=%fused_computation.14 | convolution fusion | flops 1342177280 | bytes 10354688 | tf_op jit(solution)/shard_map/dot_general | solution.py:58
  (46 shorter events, 7.8 us)
Async XLA Ops:
  8.0 8.3 %copy-start = (bf16[160,1280]{1,0:T(8,128)(2,1)S(1)}, bf16[160,1280]{1,0:T(8,128)(2,1)}, u32[]{:S(2)}) copy-start(bf16[160,1280]{1,0:T(8,128)(2,1)} %param.15) | copy-start | bytes 1228804
  8.0 4.1 %copy-start.1 = (bf16[512,1280]{1,0:T(8,128)(2,1)S(1)}, bf16[512,1280]{1,0:T(8,128)(2,1)}, u32[]{:S(2)}) copy-start(bf16[512,1280]{1,0:T(8,128)(2,1)} %param.9) | copy-start | bytes 3932164
  8.0 87.3 %all-reduce.2.cloned.1.call-start = ((), (), s32[]{:S(2)}) async-start(), calls=%async_computation.5 | async-start | bytes 2621440 | tf_op jit(solution)/shard_map/psum | solution.py:80
  10.2 3.6 %copy-start.2 = (s32[512]{0:T(512)S(1)}, s32[512]{0:T(512)}, u32[]{:S(2)}) copy-start(s32[512]{0:T(512)} %param.10) | copy-start | bytes 6148
  16.2 2.2 copy-start.4
  17.9 79.9 %all-gather.3.cloned.1.call-start = ((), (), s32[]{:S(2)}) async-start(), calls=%async_computation.6 | async-start | bytes 10813440 | tf_op jit(solution)/shard_map/all_gather | solution.py:87
  19.9 84.4 %all-to-all-start = ((s32[32,4,1]{1,2,0:T(1,128)}), s32[32,4,1]{1,2,0:T(1,128)S(1)}, u32[]{:S(2)}, u32[]{:S(2)}) async-start(s32[32,4,1]{1,2,0:T(1,128)} %bitcast), calls=%async_computation | async-start | bytes 32768 | tf_op jit(solution)/shard_map/all_to_all | solution.py:102
  97.8 18.0 %copy-start.3 = (bf16[1024]{0:T(1024)(128)(2,1)S(1)}, bf16[1024]{0:T(1024)(128)(2,1)}, u32[]{:S(2)}) copy-start(bf16[1024]{0:T(1024)(128)(2,1)} %param.17) | copy-start | bytes 6148
  104.3 20.9 %all-to-all-start.1 = ((bf16[32,4,1024]{2,1,0:T(4,128)(2,1)}), bf16[32,4,1024]{2,1,0:T(4,128)(2,1)S(1)}, u32[]{:S(2)}, u32[]{:S(2)}) async-start(bf16[32,4,1024]{2,1,0:T(4,128)(2,1)} %all_to_all.39), calls=%async_computation.1 | async-start | bytes 524288 | tf_op jit(solution)/shard_map/all_to_all | solution.py:101
  115.7 109.9 %all-gather.5.cloned.1.call-start = ((), (), s32[]{:S(2)}) async-start(), calls=%async_computation.7 | async-start | bytes 8650752 | tf_op jit(solution)/shard_map/all_gather | solution.py:121
  173.2 25.0 %all-to-all-start.3 = ((bf16[128,32,160]{0,2,1:T(8,128)(2,1)}), bf16[128,32,160]{0,2,1:T(8,128)(2,1)}, u32[]{:S(2)}, u32[]{:S(2)}) async-start(bf16[128,32,160]{0,2,1:T(8,128)(2,1)} %copy.39), calls=%async_computation.3 | async-start | bytes 2621440 | tf_op jit(solution)/shard_map/all_to_all | solution.py:83
Sparse Core Ops, SparseCore 0:
  18.0 77.2 all-reduce.1
Sparse Core Ops, SparseCore 1:
  20.9 66.7 all-gather.2
  165.3 60.3 all-gather.4
where the time goes:
time: 240 us; the launch traced here: 239 us
  waiting for transfers between devices  110 us (46%)
  matrix products  32.1 us (13%)
  blocking collectives  28.8 us (12%)
  starting transfers between devices  24.6 us (10%)
  local copies, waits for them, and re-layouts  21.8 us (9%)
  between operations  15.8 us (7%)
  other arithmetic  6.13 us (3%)
    psum x1, waiting for transfers between devices, shards(): lax.psum(partial_out.astype(jnp.bfloat16), 'tp').astype(jnp.float32)  66.8 us
    all_gather x1, waiting for transfers between devices, shards(): lax.all_gather(d_merged, 'ctx', axis=0, tiled=True)  27.4 us
    all_to_all x1, blocking collectives, shards(): lax.all_to_all(back_rows, 'ctx', split_axis=0, concat_axis=0, tiled=True)  17.6 us
    all_to_all x1, waiting for transfers between devices, shards(): lax.all_to_all(merged_in, 'ctx', split_axis=1, concat_axis=0, tiled=True)  15.3 us
    all_to_all x1, starting transfers between devices, shards(): lax.all_to_all(outgoing, 'ctx', split_axis=0, concat_axis=0, tiled=True)  11.4 us
    dot_general x3, matrix products, contract_rows(): lax.dot_general(left, right, (((0,), (0,)), ((), ())), preferred_element_...  11.4 us
    all_to_all x1, blocking collectives, sent_to_all(): return lax.all_to_all(copies, axis, split_axis=0, concat_axis=0, tiled=True)  11.2 us
    unnamed x13, local copies, waits for them, and re-layouts  10.5 us
  transfers between devices with their start and end apart: 6, of which 3 were waited for; matrix products, arithmetic and copies ran while one was open for 12% of the time, Pallas kernels for 0%

commit v1 on v0

--- a/solution.py
+++ b/solution.py
@@ -77,7 +77,9 @@
     bucket_size = slots // ctx_size
     attended = window_attention(patches, window_ids, qkv_weight)
     partial_out = jnp.dot(attended, out_weight, preferred_element_type=jnp.float32)
-    summed = lax.psum(partial_out.astype(jnp.bfloat16), "tp").astype(jnp.float32)
+    summed = jnp.sum(lax.all_gather(partial_out.astype(jnp.bfloat16), "tp"), axis=0).astype(
+        jnp.float32
+    )
     hidden = (patches.astype(jnp.float32) + summed).astype(jnp.bfloat16)
     merged_in = hidden.reshape(slots, 4 * hidden.shape[1])
     columns = lax.all_to_all(merged_in, "ctx", split_axis=1, concat_axis=0, tiled=True)

time: 240 us -> 337 us (1.40)
  waiting for transfers between devices: 110 us -> 206 us
  other arithmetic: 6.13 us -> 12.4 us
  starting transfers between devices: 24.6 us -> 18.8 us
    all_gather x0 -> x1, waiting for transfers between devices: none -> 107 us  [shards(): lax.all_gather(partial_out.astype(jnp.bfloat16), 'tp')]
    psum x1 -> x0, waiting for transfers between devices: 66.8 us -> none  [shards(): lax.psum(partial_out.astype(jnp.bfloat16), 'tp').astype(jnp.float32)]
    all_gather x1, waiting for transfers between devices: 0.03 us -> 55.7 us  [shards(): lax.all_gather(merger_weight, 'ctx', axis=0, tiled=True)]
    reduce_sum x0 -> x1, other arithmetic: none -> 6.23 us  [shards(): jnp.sum(lax.all_gather(partial_out.astype(jnp.bfloat16), 'tp'), axis=0)]
    all_to_all x1, starting transfers between devices: 11.4 us -> 5.46 us  [shards(): lax.all_to_all(outgoing, 'ctx', split_axis=0, concat_axis=0, tiled=True)]
  transfers between devices with their start and end apart: 6 -> 6, of which waited for: 3 -> 4; matrix products, arithmetic and copies ran while one was open for 12% -> 10% of each run, Pallas kernels for 0% -> 0%
where the time goes in v1:
time: 337 us; the launch traced here: 336 us
  waiting for transfers between devices  206 us (61%)
  matrix products  32.1 us (10%)
  blocking collectives  31.3 us (9%)
  local copies, waits for them, and re-layouts  21.8 us (6%)
  starting transfers between devices  18.8 us (6%)
  between operations  14 us (4%)
  other arithmetic  12.4 us (4%)
    all_gather x1, waiting for transfers between devices, shards(): lax.all_gather(partial_out.astype(jnp.bfloat16), 'tp')  107 us
    all_gather x1, waiting for transfers between devices, shards(): lax.all_gather(merger_weight, 'ctx', axis=0, tiled=True)  55.7 us
    all_gather x1, waiting for transfers between devices, shards(): lax.all_gather(d_merged, 'ctx', axis=0, tiled=True)  27.3 us
    all_to_all x1, blocking collectives, shards(): lax.all_to_all(back_rows, 'ctx', split_axis=0, concat_axis=0, tiled=True)  17.6 us
    all_to_all x1, waiting for transfers between devices, shards(): lax.all_to_all(merged_in, 'ctx', split_axis=1, concat_axis=0, tiled=True)  15.4 us
    all_to_all x1, blocking collectives, sent_to_all(): return lax.all_to_all(copies, axis, split_axis=0, concat_axis=0, tiled=True)  13.8 us
    dot_general x3, matrix products, contract_rows(): lax.dot_general(left, right, (((0,), (0,)), ((), ())), preferred_element_...  11.4 us
    unnamed x13, local copies, waits for them, and re-layouts  10.5 us
  transfers between devices with their start and end apart: 6, of which 4 were waited for; matrix products, arithmetic and copies ran while one was open for 10% of the time, Pallas kernels for 0%

profile of v1, /device:TPU:1, one launch (start us, length us, event | category | flops | bytes accessed | tf_op | source)
XLA Modules:
  0.0 336.3 jit_solution(6236507039545012990)
XLA Ops:
  7.2 2.1 convolution_convert_fusion.6
  9.3 2.0 convolution_convert_fusion.5
  15.4 1.6 convolution_convert_fusion
  19.3 8.6 %all-to-all-start = ((s32[32,4,1]{1,2,0:T(1,128)}), s32[32,4,1]{1,2,0:T(1,128)S(1)}, u32[]{:S(2)}, u32[]{:S(2)}) async-start(s32[32,4,1]{1,2,0:T(1,128)} %bitcast), calls=%async_computation | async-start | bytes 32768 | tf_op jit(solution)/shard_map/all_to_all | solution.py:104
  27.8 106.7 %all-gather.9.cloned.1.call-done = bf16[4096,1280]{1,0:T(8,128)(2,1)} async-done(((bf16[512,1280]{1,0:T(8,128)(2,1)}), bf16[4096,1280]{1,0:T(8,128)(2,1)}) %all-gather.9.cloned.1.call-update) | async-done | bytes 10485776 | tf_op jit(solution)/shard_map/all_gather | solution.py:80
  134.6 6.2 %reduce_sum.70 = bf16[512,1280]{1,0:T(8,128)(2,1)S(1)} reduce(bf16[8,512,1280]{2,1,0:T(8,128)(2,1)} %bitcast.41, bf16[]{:T(256)} %constant.69.clone.1), dimensions={0}, to_apply=%region_7.8 | reduce | flops 4587520 | bytes 11796482 | tf_op jit(solution)/shard_map/reduce_sum | solution.py:80
  140.8 1.6 add_convert_fusion
  143.3 55.7 %all-gather.5.cloned.1.call-done = bf16[5120,1024]{1,0:T(8,128)(2,1)} async-done(((bf16[160,1024]{1,0:T(8,128)(2,1)}), bf16[5120,1024]{1,0:T(8,128)(2,1)}) %all-gather.5.cloned.1.call-update) | async-done | bytes 10485776 | tf_op jit(solution)/shard_map/all_gather | solution.py:89
  199.0 5.7 %convolution_convert_fusion.2 = bf16[128,1024]{1,0:T(8,128)(2,1)S(1)} fusion(bf16[128,5120]{1,0:T(8,128)(2,1)S(1)} %reshape.118, bf16[5120,1024]{1,0:T(8,128)(2,1)} %all-gather.5.cloned.1.call-done, s32[128]{0:T(128)S(1)} %compare_select_fusion), kind=kOutput, calls=%fused_computation.19 | convolution fusion | flops 1376010240 | bytes 12059136 | tf_op jit(solution)/shard_map/dot_general | solution.py:98
  205.5 5.5 %all-to-all-start.1 = ((bf16[32,4,1024]{2,1,0:T(4,128)(2,1)}), bf16[32,4,1024]{2,1,0:T(4,128)(2,1)S(1)}, u32[]{:S(2)}, u32[]{:S(2)}) async-start(bf16[32,4,1024]{2,1,0:T(4,128)(2,1)} %all_to_all.39), calls=%async_computation.1 | async-start | bytes 524288 | tf_op jit(solution)/shard_map/all_to_all | solution.py:103
  211.2 3.9 %copy.37 = bf16[1024,1024]{0,1:T(8,128)(2,1)} copy(bf16[1024,1024]{1,0:T(8,128)(2,1)} %param.13) | data formatting | bytes 4194304 | tf_op args[4]
  215.2 4.0 %copy.36 = bf16[1024,1024]{0,1:T(8,128)(2,1)} copy(bf16[1024,1024]{1,0:T(8,128)(2,1)} %param.12) | data formatting | bytes 4194304 | tf_op args[3]
  220.7 5.6 %multiply_reduce_fusion.1 = (f32[1024]{0:T(1024)S(1)}, f32[1024]{0:T(1024)S(1)}, f32[1024,1024]{0,1:T(8,128)}) fusion(bf16[1024,1024]{0,1:T(8,128)(2,1)} %copy.37, f32[1024]{0:T(1024)S(1)} %convert_element_type.80, bf16[1024,1024]{0,1:T(8,128)(2,1)} %copy.36, bf16[128,1024]{1,0:T(8,128)(2,1)S(1)} %all_to_all.41, s32[128]{0:T(128)S(1)} %eq.74, ...), kind=kOutput, calls=%fused_computation.5 | convolution fusion | flops 276953088 | bytes 8664576 | tf_op jit(solution)/shard_map/dot_general | solution.py:108
  226.3 13.8 %all_to_all.55 = f32[8,1,2048]{2,1,0:T(1,128)S(1)} all-to-all(f32[8,1,2048]{2,1,0:T(1,128)S(1)} %broadcast_in_dim.73), channel_id=1, replica_groups=mesh['ctx'=32,'tp'=8] {'tp'}, dimensions={0} | all-to-all | bytes 131072 | tf_op jit(solution)/shard_map/all_to_all | solution.py:12
  240.1 4.3 %fusion.6 = bf16[128,1024]{1,0:T(8,128)(2,1)S(1)} fusion(f32[1024,1024]{0,1:T(8,128)} %get-tuple-element.37, bf16[1024,1024]{0,1:T(8,128)(2,1)} %copy.37, f32[1024]{0:T(1024)S(1)} %get-tuple-element.34, f32[1024]{0:T(1024)S(1)} %get-tuple-element.32, f32[1024]{0:T(1024)S(1)} %get-tuple-element.33, f32[1024]{0:T(1024)S(1)} %convert_element_type.80, ...), kind=kOutput, calls=%fused_computation.17 | convolution fusion | flops 277217280 | bytes 6570496 | tf_op jit(solution)/shard_map/dot_general | solution.py:58
  244.5 17.6 %all_to_all.56 = bf16[32,4,1024]{2,1,0:T(4,128)(2,1)S(1)} all-to-all(bf16[32,4,1024]{2,1,0:T(4,128)(2,1)S(1)} %all_to_all.47), channel_id=1, replica_groups=mesh['ctx'=32,'tp'=8] {'ctx'}, dimensions={0} | all-to-all | bytes 524288 | tf_op jit(solution)/shard_map/all_to_all | solution.py:120
  263.2 3.6 %all_to_all.43 = bf16[128,32,160]{2,1,0:T(8,128)(2,1)} reshape(bf16[512,1280]{1,0:T(8,128)(2,1)S(1)} %add_convert_fusion) | data formatting | bytes 2621440 | tf_op jit(solution)/shard_map/all_to_all | solution.py:85
  266.8 4.4 %copy.39 = bf16[128,32,160]{0,2,1:T(8,128)(2,1)} copy(bf16[128,32,160]{2,1,0:T(8,128)(2,1)} %all_to_all.43) | data formatting | bytes 2621440 | tf_op jit(solution)/shard_map/all_to_all | solution.py:85
  271.2 4.5 %all-to-all-start.3 = ((bf16[128,32,160]{0,2,1:T(8,128)(2,1)}), bf16[128,32,160]{0,2,1:T(8,128)(2,1)}, u32[]{:S(2)}, u32[]{:S(2)}) async-start(bf16[128,32,160]{0,2,1:T(8,128)(2,1)} %copy.39), calls=%async_computation.3 | async-start | bytes 2621440 | tf_op jit(solution)/shard_map/all_to_all | solution.py:85
  275.7 2.6 multiply_convert_fusion
  278.3 2.6 copy.41
  280.9 15.4 %all-to-all-done.3 = bf16[128,32,160]{0,2,1:T(8,128)(2,1)} async-done(((bf16[128,32,160]{0,2,1:T(8,128)(2,1)}), bf16[128,32,160]{0,2,1:T(8,128)(2,1)}, u32[]{:S(2)}, u32[]{:S(2)}) %all-to-all-start.3) | async-done | bytes 1310752 | tf_op jit(solution)/shard_map/all_to_all | solution.py:85
  296.3 27.3 %all-gather.7.cloned.1.call-done = bf16[4096,1024]{1,0:T(8,128)(2,1)} async-done(((bf16[128,1024]{1,0:T(8,128)(2,1)}), bf16[4096,1024]{1,0:T(8,128)(2,1)}) %all-gather.7.cloned.1.call-update) | async-done | bytes 8388624 | tf_op jit(solution)/shard_map/all_gather | solution.py:123
  323.6 6.2 %fusion.3 = f32[160,1024]{1,0:T(8,128)} fusion(bf16[4096,1024]{1,0:T(8,128)(2,1)} %all-gather.7.cloned.1.call-done, bf16[128,32,160]{0,2,1:T(8,128)(2,1)} %all-to-all-done.3), kind=kOutput, calls=%fused_computation.14 | convolution fusion | flops 1342177280 | bytes 10354688 | tf_op jit(solution)/shard_map/dot_general | solution.py:58
  (47 shorter events, 11.0 us)
Async XLA Ops:
  7.2 8.3 %copy-start = (bf16[160,1280]{1,0:T(8,128)(2,1)S(1)}, bf16[160,1280]{1,0:T(8,128)(2,1)}, u32[]{:S(2)}) copy-start(bf16[160,1280]{1,0:T(8,128)(2,1)} %param.15) | copy-start | bytes 1228804
  7.2 4.1 %copy-start.1 = (bf16[512,1280]{1,0:T(8,128)(2,1)S(1)}, bf16[512,1280]{1,0:T(8,128)(2,1)}, u32[]{:S(2)}) copy-start(bf16[512,1280]{1,0:T(8,128)(2,1)} %param.9) | copy-start | bytes 3932164
  7.2 127.4 %all-gather.9.cloned.1.call-start = ((), (), s32[]{:S(2)}) async-start(), calls=%async_computation.7 | async-start | bytes 11796480 | tf_op jit(solution)/shard_map/all_gather | solution.py:80
  9.3 3.6 %copy-start.2 = (s32[512]{0:T(512)S(1)}, s32[512]{0:T(512)}, u32[]{:S(2)}) copy-start(s32[512]{0:T(512)} %param.10) | copy-start | bytes 6148
  15.4 2.4 copy-start.4
  17.1 182.0 %all-gather.5.cloned.1.call-start = ((), (), s32[]{:S(2)}) async-start(), calls=%async_computation.5 | async-start | bytes 10813440 | tf_op jit(solution)/shard_map/all_gather | solution.py:89
  19.3 186.2 %all-to-all-start = ((s32[32,4,1]{1,2,0:T(1,128)}), s32[32,4,1]{1,2,0:T(1,128)S(1)}, u32[]{:S(2)}, u32[]{:S(2)}) async-start(s32[32,4,1]{1,2,0:T(1,128)} %bitcast), calls=%async_computation | async-start | bytes 32768 | tf_op jit(solution)/shard_map/all_to_all | solution.py:104
  143.3 67.9 %copy-start.3 = (bf16[1024]{0:T(1024)(128)(2,1)S(1)}, bf16[1024]{0:T(1024)(128)(2,1)}, u32[]{:S(2)}) copy-start(bf16[1024]{0:T(1024)(128)(2,1)} %param.17) | copy-start | bytes 6148
  205.5 15.1 %all-to-all-start.1 = ((bf16[32,4,1024]{2,1,0:T(4,128)(2,1)}), bf16[32,4,1024]{2,1,0:T(4,128)(2,1)S(1)}, u32[]{:S(2)}, u32[]{:S(2)}) async-start(bf16[32,4,1024]{2,1,0:T(4,128)(2,1)} %all_to_all.39), calls=%async_computation.1 | async-start | bytes 524288 | tf_op jit(solution)/shard_map/all_to_all | solution.py:103
  211.0 112.6 %all-gather.7.cloned.1.call-start = ((), (), s32[]{:S(2)}) async-start(), calls=%async_computation.6 | async-start | bytes 8650752 | tf_op jit(solution)/shard_map/all_gather | solution.py:123
  271.2 25.1 %all-to-all-start.3 = ((bf16[128,32,160]{0,2,1:T(8,128)(2,1)}), bf16[128,32,160]{0,2,1:T(8,128)(2,1)}, u32[]{:S(2)}, u32[]{:S(2)}) async-start(bf16[128,32,160]{0,2,1:T(8,128)(2,1)} %copy.39), calls=%async_computation.3 | async-start | bytes 2621440 | tf_op jit(solution)/shard_map/all_to_all | solution.py:85
Sparse Core Ops, SparseCore 0:
  17.2 117.3 all-gather.8
  137.1 61.8 all-gather.4
  263.3 60.2 all-gather.6
